TPU v7x, 32 devices: a whole 2x2x4 slice. The times are simulated.
32 devices in a mesh: dp: 8 (over y, x, core), mp: 4 (over z).
Axes of the slice: x: 2, y: 2, z: 4, core: 2. Of those that a mesh axis runs over, the one named last changes fastest.
Arguments:
- attn_out: bfloat16 [8192, 8192], P('dp', 'mp'), may hold values from -6 to 6
- out_weight: bfloat16 [8192, 8192], P('dp'), may hold values from -0.09375 to 0.09375
- residual: bfloat16 [8, 1024, 8192], P(None, 'mp', 'dp'), may hold values from -6 to 6
Outputs:
- layer_out: bfloat16 [8, 1024, 8192], P(None, 'mp', 'dp')
All inputs are finite; a program needn't handle non-finite values.
Results may differ from a plain program's by a relative error of at most 0.001.
Values may be sent and summed in bfloat16 or wider, within the bound.
A program may use at most 192 MiB of HBM per device.

v0:
```python
import jax
import jax.numpy as jnp
from jax import lax
from jax.sharding import PartitionSpec as P


def shards(attn_out, out_weight, residual):
    by_rows = lax.all_to_all(attn_out, "mp", split_axis=0, concat_axis=1, tiled=True)
    columns = lax.all_to_all(out_weight, "dp", split_axis=1, concat_axis=0, tiled=True)
    projected = jnp.dot(
        lax.all_gather(by_rows, "dp", axis=0, tiled=True),
        columns,
        preferred_element_type=jnp.float32,
    )
    layer_out = residual.astype(jnp.float32) + projected.reshape(residual.shape)
    return layer_out.astype(jnp.bfloat16)


def solution(mesh):
    return jax.shard_map(
        shards,
        mesh=mesh,
        in_specs=(P("dp", "mp"), P("dp", None), P(None, "mp", "dp")),
        out_specs=P(None, "mp", "dp"),
        check_vma=False,
    )
```

profile of v0, /device:TPU:0, one launch (start us, length us, event | category | flops | bytes accessed | tf_op | source)
XLA Modules:
  0.0 492.3 jit_solution(1192712560543331920)
XLA Ops:
  6.5 0.0 all-gather.2.cloned.1.call-start
  6.5 99.5 %all_to_all.38 = bf16[4,256,2048]{2,1,0:T(8,128)(2,1)S(1)} all-to-all(bf16[4,256,2048]{2,1,0:T(8,128)(2,1)} %bitcast.21), channel_id=1, replica_groups=mesh['dp'=8,'mp'=4] {'mp'}, dimensions={0} | all-to-all | bytes 8388608 | tf_op jit(solution)/shard_map/all_to_all | solution.py:8
  106.0 2.3 copy.7
  108.3 0.0 all-gather.2.cloned.1.call-update
  108.4 9.0 %copy.9 = bf16[128,8,8,1024]{3,2,0,1:T(8,128)(2,1)S(1)} copy(bf16[128,8,8,1024]{3,2,1,0:T(8,128)(2,1)} %bitcast.17) | data formatting | bytes 33554432 | tf_op jit(solution)/shard_map/all_to_all | solution.py:9
  117.4 312.1 %all_to_all.39 = bf16[1024,8,1024]{2,0,1:T(8,128)(2,1)} all-to-all(bf16[1024,8,1024]{2,0,1:T(8,128)(2,1)S(1)} %bitcast.16), channel_id=1, replica_groups=mesh['dp'=8,'mp'=4] {'dp'}, dimensions={1} | all-to-all | bytes 33554432 | tf_op jit(solution)/shard_map/all_to_all | solution.py:9
  429.5 11.2 %all-gather.2.cloned.1.call-done = bf16[2048,8192]{1,0:T(8,128)(2,1)} async-done(((bf16[256,8192]{1,0:T(8,128)(2,1)}), bf16[2048,8192]{1,0:T(8,128)(2,1)}) %all-gather.2.cloned.1.call-update) | async-done | bytes 33554448 | tf_op jit(solution)/shard_map/all_gather | solution.py:11
  440.7 44.7 %add_convert_fusion = bf16[8,256,1024]{2,1,0:T(8,128)(2,1)} fusion(bf16[8,256,1024]{2,1,0:T(8,128)(2,1)} %param.5, bf16[8,256,8192]{2,1,0:T(8,128)(2,1)} %bitcast.22, bf16[8192,1024,1]{1,0,2:T(8,128)(2,1)} %bitcast.18), kind=kOutput, calls=%fused_computation.1 | convolution fusion | flops 34366029824 | bytes 58720256 | tf_op jit(solution)/shard_map/dot_general | solution.py:10
Async XLA Ops:
  6.5 434.2 %all-gather.2.cloned.1.call-start = ((), (), s32[]{:S(2)}) async-start(), calls=%async_computation.2 | async-start | bytes 37748736 | tf_op jit(solution)/shard_map/all_gather | solution.py:11
Sparse Core Ops, SparseCore 0:
  108.5 332.2 all-gather.1
where the time goes:
time: 493 us; the launch traced here: 492 us
  blocking collectives  412 us (84%)
  matrix products  44.7 us (9%)
  between operations  13.4 us (3%)
  local copies, waits for them, and re-layouts  11.3 us (2%)
  waiting for transfers between devices  11.2 us (2%)
    all_to_all x1, blocking collectives, shards(): lax.all_to_all(out_weight, 'dp', split_axis=1, concat_axis=0, tiled=True)  312 us
    all_to_all x1, blocking collectives, shards(): lax.all_to_all(attn_out, 'mp', split_axis=0, concat_axis=1, tiled=True)  99.5 us
    dot_general x1, matrix products, shards(): jnp.dot(lax.all_gather(by_rows, 'dp', axis=0, tiled=True), columns, prefe...  44.7 us
    all_gather x1, waiting for transfers between devices, shards(): lax.all_gather(by_rows, 'dp', axis=0, tiled=True)  11.2 us
  transfers between devices with their start and end apart: 1, of which 1 were waited for; matrix products, arithmetic and copies ran while one was open for 2% of the time, Pallas kernels for 0%

commit v1 on v0

v1 whole, which is shorter than its diff:
```python
import functools

import jax
import jax.numpy as jnp
from jax import lax
from jax.experimental import pallas as pl
from jax.experimental.pallas import tpu as pltpu
from jax.sharding import PartitionSpec as P

MESH = pl.DeviceIdType.MESH
CORES = 2
TILE = 16


def flip(index, mask):
    bit = 1
    while bit <= mask:
        if mask & bit:
            index = index + (1 - 2 * ((index // bit) % 2)) * bit
        bit *= 2
    return index


def shares_of(rows, planes):
    unit = rows // (4 * planes)
    counts = [unit] * planes
    counts[0] += (rows - unit * planes) // 2
    counts[-1] += rows - sum(counts)
    chunks, start = [], 0
    for count in counts:
        cut = (count // 2 + TILE - 1) // TILE * TILE if count > 2 * unit else count
        parts = [(start, cut)]
        if count > cut:
            parts.append((start + cut, count - cut))
        chunks.append(parts)
        start += count
    return chunks


def merged(first, second):
    out, a, b = [], list(first), list(second)
    total = max(len(a), len(b))
    for step in range(total):
        for tasks in (a, b):
            lo, hi = step * len(tasks) // total, (step + 1) * len(tasks) // total
            out.extend(tasks[lo:hi])
    return out


def gather_kernel(devices, planes, a_ref, w_ref, rows_ref, cols_ref, a_stage, w_stage,
                  az_s, az_r, ap_s, ap_r, ac_s, ac_r, wp_s, wp_r, wz_s, wz_r, loc):
    chips = devices // CORES
    tok, heads = a_ref.shape[0] // planes, a_ref.shape[1]
    depth, width = w_ref.shape[0], cols_ref.shape[1]
    half = tok // 2
    d = lax.axis_index("dp")
    z = lax.axis_index("mp")
    q, c = d // CORES, d % CORES
    chunks = shares_of(depth, planes)
    bits = [1 << k for k in range(chips.bit_length() - 1)]

    def chip_dev(mask, cross=0):
        return flip(q, mask) * CORES + flip(c, cross)

    def copy(src, dst, s, r, dp, mp):
        return pltpu.make_async_remote_copy(
            src_ref=src, dst_ref=dst, send_sem=s, recv_sem=r,
            device_id={"dp": dp, "mp": mp}, device_id_type=MESH)

    barrier = pltpu.get_barrier_semaphore()
    sources = [(m, x) for m in range(chips) for x in range(CORES) if (m, x) != (0, 0)]
    for m, x in sources:
        pl.semaphore_signal(barrier, inc=1, device_id={"dp": chip_dev(m, x), "mp": z}, device_id_type=MESH)
    for step in range(1, planes):
        pl.semaphore_signal(barrier, inc=1, device_id={"dp": d, "mp": lax.rem(z + step, planes)}, device_id_type=MESH)
    pl.semaphore_wait(barrier, len(sources) + planes - 1)

    def part(owner, j, h):
        return rows_ref.at[pl.ds(pl.multiple_of(owner * tok + h * half, TILE), half), pl.ds(j * heads, heads)]

    def wcols(dev):
        return pl.ds(pl.multiple_of(dev * width, 128), width)

    def wdst(dev, start, count):
        return cols_ref.at[pl.ds(pl.multiple_of(dev * depth + start, TILE), count), :]

    def run(me):
        sends, recvs = [], []

        def go(cp):
            cp.start()
            sends.append(cp)

        others = sorted((m for m in range(planes) if m != me), key=lambda m: -abs(m - me))
        for m in others:
            go(copy(a_ref.at[pl.ds(m * tok, tok), :],
                    rows_ref.at[pl.ds(pl.multiple_of(d * tok, TILE), tok), pl.ds(me * heads, heads)],
                    az_s.at[m], az_r.at[me], d, m))
        a_in = pltpu.make_async_copy(a_ref.at[pl.ds(me * tok, tok), :], a_stage, loc.at[0])
        w_in = pltpu.make_async_copy(w_ref.at[:, wcols(d)], w_stage, loc.at[1])
        a_in.start()
        w_in.start()

        nchunk = len(chunks[me])
        for k, (start, count) in enumerate(chunks[me]):
            for m, x in sources:
                if m:
                    to = chip_dev(m, x)
                    i = m * CORES + x
                    go(copy(w_ref.at[pl.ds(start, count), wcols(to)], wdst(d, start, count),
                            wp_s.at[i, k], wp_r.at[i, k], to, me))
        mate = chip_dev(0, 1)
        go(copy(w_ref.at[:, wcols(mate)], wdst(d, 0, depth), wp_s.at[1, 0], wp_r.at[1, 0], mate, me))

        def order(h):
            return bits if h == 0 else bits[::-1]

        def held_before(h, k):
            spans = [0]
            for bit in order(h)[:k]:
                spans += [u ^ bit for u in spans]
            return spans

        def to_mate(u, j, h, src=None):
            piece = part(chip_dev(u), j, h)
            go(copy(piece if src is None else src, piece, ac_s.at[u, j, h], ac_r.at[u, j, h], mate, me))

        def forward(u, j, h, k0, src=None):
            piece = part(chip_dev(u), j, h)
            for bit in order(h)[k0:]:
                go(copy(piece if src is None else src, piece, ap_s.at[u ^ bit, j, h], ap_r.at[u ^ bit, j, h],
                        chip_dev(bit), me))
            to_mate(u, j, h, src)

        for h in range(2):
            forward(0, me, h, 0, a_ref.at[pl.ds(me * tok + h * half, half), :])
        for j in others[::-1]:
            whole = rows_ref.at[pl.ds(pl.multiple_of(d * tok, TILE), tok), pl.ds(j * heads, heads)]
            copy(whole, whole, az_s.at[j], az_r.at[j], d, j).wait_recv()
            for h in range(2):
                forward(0, j, h, 0)

        def wait_w(sem, i, start, count, at):
            piece = wdst(chip_dev(i // CORES, i % CORES), start, count)
            copy(piece, piece, sem, sem, at, me).wait_recv()
            return piece

        def send_w(piece, origin, i, k, target):
            go(copy(piece, piece, wz_s.at[origin, i, k, int(target > me)], wz_r.at[origin, i, k], d, target))

        far = [m * CORES + x for m, x in sources if m]

        def share(k, i):
            start, count = chunks[me][k]
            piece = wait_w(wp_r.at[i, k], i, start, count, mate)
            for target in (me - 1, me + 1):
                if 0 <= target < planes:
                    send_w(piece, me, i, k, target)

        for k in range(nchunk):
            for i in far:
                share(k, i)

        def later(u, j, h, k0):
            piece = part(chip_dev(u), j, h)
            copy(piece, piece, ap_s.at[u, j, h], ap_r.at[u, j, h], mate, me).wait_recv()
            forward(u, j, h, k0)

        def pass_on(origin, i, k):
            start, count = chunks[origin][k]
            piece = wait_w(wz_r.at[origin, i, k], i, start, count, mate)
            target = me + (1 if origin < me else -1)
            if 0 <= target < planes:
                send_w(piece, origin, i, k, target)

        token_tasks = []
        js = [me] + others[::-1]
        for stage in range(len(bits)):
            for j in js:
                for h in range(2):
                    bit = order(h)[stage]
                    for u in held_before(h, stage):
                        token_tasks.append(functools.partial(later, u ^ bit, j, h, stage + 1))
        weight_tasks = []
        for dist in range(1, planes):
            origins = [o for o in (me - dist, me + dist) if 0 <= o < planes]
            for k in range(2):
                for i in far:
                    for o in origins:
                        if k < len(chunks[o]):
                            weight_tasks.append(functools.partial(pass_on, o, i, k))
        for task in merged(token_tasks, weight_tasks):
            task()

        a_in.wait()
        a_out = pltpu.make_async_copy(
            a_stage, rows_ref.at[pl.ds(pl.multiple_of(d * tok, TILE), tok), pl.ds(me * heads, heads)], loc.at[0])
        a_out.start()
        w_in.wait()
        w_out = pltpu.make_async_copy(w_stage, wdst(d, 0, depth), loc.at[1])
        w_out.start()
        piece = wdst(mate, 0, depth)
        copy(piece, piece, wp_s.at[1, 0], wp_r.at[1, 0], mate, me).wait_recv()
        for u in range(chips):
            for j in range(planes):
                for h in range(2):
                    piece = part(chip_dev(u, 1), j, h)
                    copy(piece, piece, ac_s.at[u, j, h], ac_r.at[u, j, h], mate, me).wait_recv()
        for cp in sends:
            cp.wait_send()
        a_out.wait()
        w_out.wait()

    for me in range(planes):
        pl.when(z == me)(functools.partial(run, me))


def shards(devices, planes, attn_out, out_weight, residual):
    chips = devices // CORES
    tok, heads = attn_out.shape[0] // planes, attn_out.shape[1]
    depth, width = out_weight.shape[0], out_weight.shape[1] // devices
    sem = pltpu.SemaphoreType.DMA
    rows, columns = pl.pallas_call(
        functools.partial(gather_kernel, devices, planes),
        out_shape=(
            jax.ShapeDtypeStruct((devices * tok, planes * heads), attn_out.dtype),
            jax.ShapeDtypeStruct((devices * depth, width), out_weight.dtype),
        ),
        in_specs=[pl.BlockSpec(memory_space=pl.ANY)] * 2,
        out_specs=[pl.BlockSpec(memory_space=pl.ANY)] * 2,
        scratch_shapes=[
            pltpu.VMEM((tok, heads), attn_out.dtype),
            pltpu.VMEM((depth, width), out_weight.dtype),
            sem((planes,)), sem((planes,)),
            sem((chips, planes, 2)), sem((chips, planes, 2)),
            sem((chips, planes, 2)), sem((chips, planes, 2)),
            sem((devices, 2)), sem((devices, 2)),
            sem((planes, devices, 2, 2)), sem((planes, devices, 2)),
            sem((2,)),
        ],
        compiler_params=pltpu.CompilerParams(collective_id=0, has_side_effects=True),
    )(attn_out, out_weight)
    projected = jnp.dot(rows, columns, preferred_element_type=jnp.float32)
    layer_out = residual.astype(jnp.float32) + projected.reshape(residual.shape)
    return layer_out.astype(jnp.bfloat16)


def solution(mesh):
    return jax.shard_map(
        functools.partial(shards, mesh.shape["dp"], mesh.shape["mp"]),
        mesh=mesh,
        in_specs=(P("dp", "mp"), P("dp", None), P(None, "mp", "dp")),
        out_specs=P(None, "mp", "dp"),
        check_vma=False,
    )
```

time: 493 us -> 363 us (0.74)
  blocking collectives: 412 us -> 0 us
  Pallas kernels: 0 us -> 318 us
  between operations: 13.4 us -> 0.03 us
  local copies, waits for them, and re-layouts: 11.3 us -> 0.01 us
  waiting for transfers between devices: 11.2 us -> 0 us
    all_to_all x2 -> x0, blocking collectives: 412 us -> none  [the longest x1 312 us: shards(): lax.all_to_all(out_weight, 'dp', split_axis=1, concat_axis=0, tiled=True)]
    pallas_call x0 -> x1, Pallas kernels: none -> 318 us  [shards(): pl.pallas_call(functools.partial(gather_kernel, devices, planes), out_sha...]
    all_to_all x2 -> x0, local copies, waits for them, and re-layouts: 11.3 us -> none  [the longest x1 9.01 us: shards(): lax.all_to_all(out_weight, 'dp', split_axis=1, concat_axis=0, tiled=True)]
    all_gather x1 -> x0, waiting for transfers between devices: 11.2 us -> none  [shards(): lax.all_gather(by_rows, 'dp', axis=0, tiled=True)]
  transfers between devices with their start and end apart: 1 -> 0, of which waited for: 1 -> 0; matrix products, arithmetic and copies ran while one was open for 2% -> 0% of each run, Pallas kernels for 0% -> 0%
where the time goes in v1:
time: 363 us; the launch traced here: 362 us
  Pallas kernels  318 us (88%)
  matrix products  40.4 us (11%)
  other arithmetic  3.71 us (1%)
    pallas_call x1, Pallas kernels, shards(): pl.pallas_call(functools.partial(gather_kernel, devices, planes), out_sha...  318 us
    dot_general x1, matrix products, shards(): projected = jnp.dot(rows, columns, preferred_element_type=jnp.float32)  40.4 us

profile of v1, /device:TPU:0, one launch (start us, length us, event | category | flops | bytes accessed | tf_op | source)
XLA Modules:
  0.0 362.5 jit_solution(7005903101285675166)
XLA Ops:
  0.0 318.4 %shard_map.37 = (bf16[2048,8192]{1,0:T(8,128)(2,1)}, bf16[8192,1024]{1,0:T(8,128)(2,1)}) custom-call(bf16[1024,2048]{1,0:T(8,128)(2,1)} %a_ref.1, bf16[1024,8192]{1,0:T(8,128)(2,1)} %w_ref.1), custom_call_target="tpu_custom_call" | custom-call | tf_op jit(solution)/shard_map/pallas_call | solution.py:223
  318.4 0.0 copy-start
  318.4 40.4 %fusion = f32[2048,1024]{1,0:T(8,128)S(1)} fusion(bf16[2048,8192]{1,0:T(8,128)(2,1)} %get-tuple-element.7, bf16[8192,1024]{1,0:T(8,128)(2,1)} %get-tuple-element.8), kind=kOutput, calls=%fused_computation.1 | convolution fusion | flops 34359738368 | bytes 58720256 | tf_op jit(solution)/shard_map/dot_general | solution.py:243
  358.8 0.0 copy-done
  358.8 3.7 %add_convert_fusion = bf16[8,256,1024]{2,1,0:T(8,128)(2,1)} fusion(f32[8,256,1024]{2,1,0:T(8,128)S(1)} %bitcast.3, bf16[8,256,1024]{2,1,0:T(8,128)(2,1)S(1)} %copy-done), kind=kLoop, calls=%fused_computation | loop fusion | flops 6291456 | bytes 16777216 | tf_op jit(solution)/shard_map/convert_element_type | solution.py:245
Async XLA Ops:
  318.4 40.4 %copy-start = (bf16[8,256,1024]{2,1,0:T(8,128)(2,1)S(1)}, bf16[8,256,1024]{2,1,0:T(8,128)(2,1)}, u32[]{:S(2)}) copy-start(bf16[8,256,1024]{2,1,0:T(8,128)(2,1)} %param.5) | copy-start | bytes 12582916

commit v2 on v1

--- a/solution.py
+++ b/solution.py
@@ -37,16 +37,6 @@
     return chunks
 
 
-def merged(first, second):
-    out, a, b = [], list(first), list(second)
-    total = max(len(a), len(b))
-    for step in range(total):
-        for tasks in (a, b):
-            lo, hi = step * len(tasks) // total, (step + 1) * len(tasks) // total
-            out.extend(tasks[lo:hi])
-    return out
-
-
 def gather_kernel(devices, planes, a_ref, w_ref, rows_ref, cols_ref, a_stage, w_stage,
                   az_s, az_r, ap_s, ap_r, ac_s, ac_r, wp_s, wp_r, wz_s, wz_r, loc):
     chips = devices // CORES
@@ -134,11 +124,18 @@
 
         for h in range(2):
             forward(0, me, h, 0, a_ref.at[pl.ds(me * tok + h * half, half), :])
-        for j in others[::-1]:
+        share_of = [sum(count for _, count in parts) / depth for parts in chunks]
+        wait_for = []
+
+        def along(j):
             whole = rows_ref.at[pl.ds(pl.multiple_of(d * tok, TILE), tok), pl.ds(j * heads, heads)]
             copy(whole, whole, az_s.at[j], az_r.at[j], d, j).wait_recv()
             for h in range(2):
                 forward(0, j, h, 0)
+
+        line = planes if 0 < me < planes - 1 else planes - 1
+        for rank, j in enumerate(others[::-1]):
+            wait_for.append((line * (rank + 1) / len(others), functools.partial(along, j)))
 
         def wait_w(sem, i, start, count, at):
             piece = wdst(chip_dev(i // CORES, i % CORES), start, count)
@@ -157,9 +154,10 @@
                 if 0 <= target < planes:
                     send_w(piece, me, i, k, target)
 
-        for k in range(nchunk):
-            for i in far:
-                share(k, i)
+        inside = [(k, i) for k in range(nchunk) for i in far]
+        fetched = 2 * planes * share_of[me]
+        for p, (k, i) in enumerate(inside):
+            wait_for.append((fetched * (p + 1) / len(inside), functools.partial(share, k, i)))
 
         def later(u, j, h, k0):
             piece = part(chip_dev(u), j, h)
@@ -173,23 +171,23 @@
             if 0 <= target < planes:
                 send_w(piece, origin, i, k, target)
 
-        token_tasks = []
         js = [me] + others[::-1]
         for stage in range(len(bits)):
-            for j in js:
+            for rank, j in enumerate(js):
                 for h in range(2):
                     bit = order(h)[stage]
                     for u in held_before(h, stage):
-                        token_tasks.append(functools.partial(later, u ^ bit, j, h, stage + 1))
-        weight_tasks = []
-        for dist in range(1, planes):
-            origins = [o for o in (me - dist, me + dist) if 0 <= o < planes]
-            for k in range(2):
-                for i in far:
-                    for o in origins:
-                        if k < len(chunks[o]):
-                            weight_tasks.append(functools.partial(pass_on, o, i, k))
-        for task in merged(token_tasks, weight_tasks):
+                        at = fetched + 1.5 * planes * (rank * 2 + h + 1) / (2 * len(js)) + 0.5 * stage
+                        wait_for.append((at, functools.partial(later, u ^ bit, j, h, stage + 1)))
+        for o in range(planes):
+            if o != me:
+                dist = abs(o - me)
+                pieces = [(k, i) for k in range(len(chunks[o])) for i in far]
+                first = planes - 1 if dist == 1 else planes + 3 * share_of[1]
+                for p, (k, i) in enumerate(pieces):
+                    at = first + 3 * planes * share_of[o] * (p + 1) / len(pieces) + 0.3 * dist
+                    wait_for.append((at, functools.partial(pass_on, o, i, k)))
+        for _, task in sorted(wait_for, key=lambda entry: entry[0]):
             task()
 
         a_in.wait()

time: 363 us -> 367 us (1.011)
  Pallas kernels: 318 us -> 323 us
    pallas_call x1, Pallas kernels: 318 us -> 323 us  [shards(): pl.pallas_call(functools.partial(gather_kernel, devices, planes), out_sha...]
where the time goes in v2:
time: 367 us
  Pallas kernels  323 us (88%)
  matrix products  40.4 us (11%)
  other arithmetic  3.71 us (1%)
    pallas_call x1, Pallas kernels, shards(): pl.pallas_call(functools.partial(gather_kernel, devices, planes), out_sha...  323 us
    dot_general x1, matrix products, shards(): projected = jnp.dot(rows, columns, preferred_element_type=jnp.float32)  40.4 us

profile of v2, /device:TPU:0, one launch (start us, length us, event | category | flops | bytes accessed | tf_op | source)
XLA Modules:
  0.0 366.8 jit_solution(9576898248147681247)
XLA Ops:
  0.0 322.6 %shard_map.37 = (bf16[2048,8192]{1,0:T(8,128)(2,1)}, bf16[8192,1024]{1,0:T(8,128)(2,1)}) custom-call(bf16[1024,2048]{1,0:T(8,128)(2,1)} %a_ref.1, bf16[1024,8192]{1,0:T(8,128)(2,1)} %w_ref.1), custom_call_target="tpu_custom_call" | custom-call | tf_op jit(solution)/shard_map/pallas_call | solution.py:221
  322.6 0.0 copy-start
  322.6 40.4 %fusion = f32[2048,1024]{1,0:T(8,128)S(1)} fusion(bf16[2048,8192]{1,0:T(8,128)(2,1)} %get-tuple-element.7, bf16[8192,1024]{1,0:T(8,128)(2,1)} %get-tuple-element.8), kind=kOutput, calls=%fused_computation.1 | convolution fusion | flops 34359738368 | bytes 58720256 | tf_op jit(solution)/shard_map/dot_general | solution.py:241
  363.0 0.0 copy-done
  363.0 3.7 %add_convert_fusion = bf16[8,256,1024]{2,1,0:T(8,128)(2,1)} fusion(f32[8,256,1024]{2,1,0:T(8,128)S(1)} %bitcast.3, bf16[8,256,1024]{2,1,0:T(8,128)(2,1)S(1)} %copy-done), kind=kLoop, calls=%fused_computation | loop fusion | flops 6291456 | bytes 16777216 | tf_op jit(solution)/shard_map/convert_element_type | solution.py:243
Async XLA Ops:
  322.6 40.4 %copy-start = (bf16[8,256,1024]{2,1,0:T(8,128)(2,1)S(1)}, bf16[8,256,1024]{2,1,0:T(8,128)(2,1)}, u32[]{:S(2)}) copy-start(bf16[8,256,1024]{2,1,0:T(8,128)(2,1)} %param.5) | copy-start | bytes 12582916

commit v3 on v2

--- a/solution.py
+++ b/solution.py
@@ -81,11 +81,11 @@
             cp.start()
             sends.append(cp)
 
-        others = sorted((m for m in range(planes) if m != me), key=lambda m: -abs(m - me))
+        others = sorted((m for m in range(planes) if m != me), key=lambda m: abs(m - me))
         for m in others:
-            go(copy(a_ref.at[pl.ds(m * tok, tok), :],
-                    rows_ref.at[pl.ds(pl.multiple_of(d * tok, TILE), tok), pl.ds(me * heads, heads)],
-                    az_s.at[m], az_r.at[me], d, m))
+            for h in range(2):
+                go(copy(a_ref.at[pl.ds(m * tok + h * half, half), :], part(d, me, h),
+                        az_s.at[m, h], az_r.at[me, h], d, m))
         a_in = pltpu.make_async_copy(a_ref.at[pl.ds(me * tok, tok), :], a_stage, loc.at[0])
         w_in = pltpu.make_async_copy(w_ref.at[:, wcols(d)], w_stage, loc.at[1])
         a_in.start()
@@ -127,15 +127,16 @@
         share_of = [sum(count for _, count in parts) / depth for parts in chunks]
         wait_for = []
 
-        def along(j):
-            whole = rows_ref.at[pl.ds(pl.multiple_of(d * tok, TILE), tok), pl.ds(j * heads, heads)]
-            copy(whole, whole, az_s.at[j], az_r.at[j], d, j).wait_recv()
+        def along(j, h):
+            piece = part(d, j, h)
+            copy(piece, piece, az_s.at[j, h], az_r.at[j, h], d, j).wait_recv()
+            forward(0, j, h, 0)
+
+        line = planes if 0 < me < planes - 1 else planes - 1
+        for rank, j in enumerate(others):
             for h in range(2):
-                forward(0, j, h, 0)
-
-        line = planes if 0 < me < planes - 1 else planes - 1
-        for rank, j in enumerate(others[::-1]):
-            wait_for.append((line * (rank + 1) / len(others), functools.partial(along, j)))
+                at = line * (rank + 0.5 * (h + 1)) / len(others)
+                wait_for.append((at, functools.partial(along, j, h)))
 
         def wait_w(sem, i, start, count, at):
             piece = wdst(chip_dev(i // CORES, i % CORES), start, count)
@@ -171,7 +172,7 @@
             if 0 <= target < planes:
                 send_w(piece, origin, i, k, target)
 
-        js = [me] + others[::-1]
+        js = [me] + others
         for stage in range(len(bits)):
             for rank, j in enumerate(js):
                 for h in range(2):
@@ -229,7 +230,7 @@
         scratch_shapes=[
             pltpu.VMEM((tok, heads), attn_out.dtype),
             pltpu.VMEM((depth, width), out_weight.dtype),
-            sem((planes,)), sem((planes,)),
+            sem((planes, 2)), sem((planes, 2)),
             sem((chips, planes, 2)), sem((chips, planes, 2)),
             sem((chips, planes, 2)), sem((chips, planes, 2)),
             sem((devices, 2)), sem((devices, 2)),

time: 367 us -> 313 us (0.85)
  Pallas kernels: 323 us -> 266 us
    pallas_call x1, Pallas kernels: 323 us -> 266 us  [shards(): pl.pallas_call(functools.partial(gather_kernel, devices, planes), out_sha...]
where the time goes in v3:
time: 313 us; the launch traced here: 311 us
  Pallas kernels  266 us (85%)
  matrix products  40.4 us (13%)
  other arithmetic  3.71 us (1%)
    pallas_call x1, Pallas kernels, shards(): pl.pallas_call(functools.partial(gather_kernel, devices, planes), out_sha...  266 us
    dot_general x1, matrix products, shards(): projected = jnp.dot(rows, columns, preferred_element_type=jnp.float32)  40.4 us

profile of v3, /device:TPU:0, one launch (start us, length us, event | category | flops | bytes accessed | tf_op | source)
XLA Modules:
  0.0 310.6 jit_solution(13409649777470852254)
XLA Ops:
  0.0 266.4 %shard_map.37 = (bf16[2048,8192]{1,0:T(8,128)(2,1)}, bf16[8192,1024]{1,0:T(8,128)(2,1)}) custom-call(bf16[1024,2048]{1,0:T(8,128)(2,1)} %a_ref.1, bf16[1024,8192]{1,0:T(8,128)(2,1)} %w_ref.1), custom_call_target="tpu_custom_call" | custom-call | tf_op jit(solution)/shard_map/pallas_call | solution.py:222
  266.4 0.0 copy-start
  266.5 40.4 %fusion = f32[2048,1024]{1,0:T(8,128)S(1)} fusion(bf16[2048,8192]{1,0:T(8,128)(2,1)} %get-tuple-element.7, bf16[8192,1024]{1,0:T(8,128)(2,1)} %get-tuple-element.8), kind=kOutput, calls=%fused_computation.1 | convolution fusion | flops 34359738368 | bytes 58720256 | tf_op jit(solution)/shard_map/dot_general | solution.py:242
  306.8 0.0 copy-done
  306.8 3.7 %add_convert_fusion = bf16[8,256,1024]{2,1,0:T(8,128)(2,1)} fusion(f32[8,256,1024]{2,1,0:T(8,128)S(1)} %bitcast.3, bf16[8,256,1024]{2,1,0:T(8,128)(2,1)S(1)} %copy-done), kind=kLoop, calls=%fused_computation | loop fusion | flops 6291456 | bytes 16777216 | tf_op jit(solution)/shard_map/convert_element_type | solution.py:244
Async XLA Ops:
  266.4 40.4 %copy-start = (bf16[8,256,1024]{2,1,0:T(8,128)(2,1)S(1)}, bf16[8,256,1024]{2,1,0:T(8,128)(2,1)}, u32[]{:S(2)}) copy-start(bf16[8,256,1024]{2,1,0:T(8,128)(2,1)} %param.5) | copy-start | bytes 12582916
